TPU v7x, 32 devices: a whole 2x2x4 slice. The times are simulated.
32 devices in a mesh: col: 16 (over z, y, x), row: 2 (over core).
Axes of the slice: x: 2, y: 2, z: 4, core: 2. Of those that a mesh axis runs over, the one named last changes fastest.
Arguments:
- kernel: float32 [512, 131072], P('row', 'col'), may hold values from -0.0234375 to 0.0234375
- slip_deficit: float32 [64, 131072], P(None, ('col', 'row')), may hold values from -6 to 6
- loading: float32 [512], P('row'), may hold values from -4 to 4
- direct_effect: float32 [512], P('row'), may hold values from 1 to 4
- log_state: float32 [64, 512], P(None, 'row'), may hold values from -1 to 1
Outputs:
- slip_rate: float32 [64, 512], P(None, 'row')
- next_state: float32 [64, 512], P(None, 'row')
All inputs are finite; a program needn't handle non-finite values. Where the computation divides by a largest or mean magnitude, that divisor is 1e-20 or more.
Results may differ from a plain program's by a relative error of at most 0.00013.
Values sent between devices are 32-bit elements; how exact they have to be, the bound alone decides.
A program may use at most 64 MiB of HBM per device.

v0:
```python
import jax
import jax.numpy as jnp
from jax import lax
from jax.sharding import PartitionSpec as P


def friction(stress, direct_effect, log_state):
    return 2.0 * jnp.exp(-log_state) * jnp.sinh(stress / direct_effect[None, :])


def evolve(log_state, slip_rate, peak_rate):
    step_size = 1.0 / (peak_rate + 1e-06)
    return log_state + step_size[:, None] * (jnp.exp(-log_state) - jnp.abs(slip_rate))


def on_device(kernel, slip_deficit, loading, direct_effect, log_state):
    partial_stress = lax.dot_general(
        lax.all_gather(slip_deficit, "row", axis=1, tiled=True),
        kernel,
        (((1,), (1,)), ((), ())),
        precision=lax.Precision.HIGHEST,
        preferred_element_type=jnp.float32,
    )
    stress = lax.psum(partial_stress, "col") + loading[None, :]
    slip_rate = friction(stress, direct_effect, log_state)
    peak_rate = lax.pmax(jnp.max(jnp.abs(slip_rate), axis=1), "row")
    next_state = evolve(log_state, slip_rate, peak_rate)
    return (slip_rate, next_state)


def solution(mesh):
    return jax.shard_map(
        on_device,
        mesh=mesh,
        in_specs=(P("row", "col"), P(None, ("col", "row")), P("row"), P("row"), P(None, "row")),
        out_specs=(P(None, "row"), P(None, "row")),
        check_vma=False,
    )
```

profile of v0, /device:TPU:0, one launch (start us, length us, event | category | flops | bytes accessed | tf_op | source)
XLA Modules:
  0.0 151.2 jit_solution(1238443934083582144)
XLA Ops:
  7.2 0.0 copy-start
  7.2 0.0 copy-start.2
  7.2 0.0 copy-start.3
  7.2 0.0 all-gather.2.cloned.1.call-start
  7.2 0.7 all-gather.2.cloned.1.call-update
  7.9 0.0 all-reduce.2.cloned.1.call-start
  8.0 14.9 %all-gather.2.cloned.1.call-done = f32[64,8192]{1,0:T(8,128)} async-done(((f32[64,4096]{1,0:T(8,128)}), f32[64,8192]{1,0:T(8,128)}) %all-gather.2.cloned.1.call-update) | async-done | bytes 2097168 | tf_op jit(solution)/shard_map/all_gather | solution.py:18
  22.9 12.4 %fusion.4 = f32[64,256]{1,0:T(8,128)} fusion(f32[64,8192]{1,0:T(8,128)} %all-gather.2.cloned.1.call-done, f32[256,8192]{1,0:T(8,128)} %param.5), kind=kOutput, calls=%fused_computation.9 | convolution fusion | flops 1610612736 | bytes 10551296 | tf_op jit(solution)/shard_map/dot_general | solution.py:17
  35.3 0.0 all-reduce.2.cloned.1.call-update
  35.3 104.8 %all-reduce.2.cloned.1.call-done = f32[64,256]{1,0:T(8,128)} async-done(((f32[64,256]{1,0:T(8,128)}), f32[64,256]{1,0:T(8,128)}) %all-reduce.2.cloned.1.call-update) | async-done | bytes 65552 | tf_op jit(solution)/shard_map/psum | solution.py:24
  140.1 0.0 copy-done
  140.1 0.0 copy-done.2
  140.1 0.0 copy-done.3
  140.1 1.0 abs_reduce_fusion
  141.1 0.0 copy-start.1
  141.1 2.5 %pmax.7 = f32[64]{0:T(128)S(1)} all-reduce(f32[64]{0:T(128)S(1)} %get-tuple-element.2), channel_id=1, replica_groups=mesh['col'=16,'row'=2] {'row'}, use_global_device_ids=true, to_apply=%region_2.0 | all-reduce | flops 64 | bytes 512 | tf_op jit(solution)/shard_map/pmax | solution.py:26
  143.6 0.7 multiply_add_fusion
  144.3 0.0 copy-done.1
  (1 shorter events, 0.0 us)
Async XLA Ops:
  7.2 132.9 %copy-start = (f32[64,256]{1,0:T(8,128)S(1)}, f32[64,256]{1,0:T(8,128)}, u32[]{:S(2)}) copy-start(f32[64,256]{1,0:T(8,128)} %param.9) | copy-start | bytes 196612
  7.2 132.9 %copy-start.2 = (f32[256]{0:T(256)S(1)}, f32[256]{0:T(256)}, u32[]{:S(2)}) copy-start(f32[256]{0:T(256)} %param.8) | copy-start | bytes 3076
  7.2 132.9 %copy-start.3 = (f32[256]{0:T(256)S(1)}, f32[256]{0:T(256)}, u32[]{:S(2)}) copy-start(f32[256]{0:T(256)} %param.7) | copy-start | bytes 3076
  7.2 15.7 %all-gather.2.cloned.1.call-start = ((), (), s32[]{:S(2)}) async-start(), calls=%async_computation | async-start | bytes 3145728 | tf_op jit(solution)/shard_map/all_gather | solution.py:18
  7.9 132.2 %all-reduce.2.cloned.1.call-start = ((), (), s32[]{:S(2)}) async-start(), calls=%async_computation.1 | async-start | bytes 131072 | tf_op jit(solution)/shard_map/psum | solution.py:24
  141.1 3.2 %copy-start.1 = (f32[64,256]{1,0:T(8,128)}, f32[64,256]{1,0:T(8,128)S(1)}, u32[]{:S(2)}) copy-start(f32[64,256]{1,0:T(8,128)S(1)} %get-tuple-element.3) | copy-start | bytes 196612
Sparse Core Ops, SparseCore 0:
  9.5 13.2 all-gather.1
  35.4 104.6 all-reduce.1
where the time goes:
time: 151 us
  waiting for transfers between devices  120 us (79%)
  between operations  14.1 us (9%)
  matrix products  12.4 us (8%)
  blocking collectives  2.47 us (2%)
  other arithmetic  1.74 us (1%)
    psum x1, waiting for transfers between devices, on_device(): stress = lax.psum(partial_stress, 'col') + loading[None, :]  105 us
    all_gather x1, waiting for transfers between devices, on_device(): lax.all_gather(slip_deficit, 'row', axis=1, tiled=True)  14.9 us
    dot_general x1, matrix products, on_device(): lax.dot_general(lax.all_gather(slip_deficit, 'row', axis=1, tiled=True),...  12.4 us
  transfers between devices with their start and end apart: 2, of which 2 were waited for; matrix products, arithmetic and copies ran while one was open for 0% of the time, Pallas kernels for 0%

commit v1 on v0

--- a/solution.py
+++ b/solution.py
@@ -2,6 +2,11 @@
 import jax.numpy as jnp
 from jax import lax
 from jax.sharding import PartitionSpec as P
+
+
+def points_wrap(sheet, mesh_name):
+    e_next = jnp.sum(lax.all_gather(sheet, mesh_name), 0)
+    return e_next
 
 
 def friction(stress, direct_effect, log_state):
@@ -21,7 +26,7 @@
         precision=lax.Precision.HIGHEST,
         preferred_element_type=jnp.float32,
     )
-    stress = lax.psum(partial_stress, "col") + loading[None, :]
+    stress = points_wrap(partial_stress, "col") + loading[None, :]
     slip_rate = friction(stress, direct_effect, log_state)
     peak_rate = lax.pmax(jnp.max(jnp.abs(slip_rate), axis=1), "row")
     next_state = evolve(log_state, slip_rate, peak_rate)

time: 151 us -> 103 us (0.68)
  waiting for transfers between devices: 120 us -> 72 us
    psum x1 -> x0, waiting for transfers between devices: 105 us -> none  [on_device(): stress = lax.psum(partial_stress, 'col') + loading[None, :]]
    all_gather x0 -> x1, waiting for transfers between devices: none -> 56.4 us  [points_wrap(): e_next = jnp.sum(lax.all_gather(sheet, mesh_name), 0)]
where the time goes in v1:
time: 103 us
  waiting for transfers between devices  72 us (70%)
  between operations  14.1 us (14%)
  matrix products  12.4 us (12%)
  blocking collectives  2.47 us (2%)
  other arithmetic  2.19 us (2%)
    all_gather x1, waiting for transfers between devices, points_wrap(): e_next = jnp.sum(lax.all_gather(sheet, mesh_name), 0)  56.4 us
    all_gather x1, waiting for transfers between devices, on_device(): lax.all_gather(slip_deficit, 'row', axis=1, tiled=True)  14.9 us
    dot_general x1, matrix products, on_device(): lax.dot_general(lax.all_gather(slip_deficit, 'row', axis=1, tiled=True),...  12.4 us
    pmax x1, blocking collectives, on_device(): peak_rate = lax.pmax(jnp.max(jnp.abs(slip_rate), axis=1), 'row')  2.47 us
  transfers between devices with their start and end apart: 2, of which 2 were waited for; matrix products, arithmetic and copies ran while one was open for 0% of the time, Pallas kernels for 0%

profile of v1, /device:TPU:0, one launch (start us, length us, event | category | flops | bytes accessed | tf_op | source)
XLA Modules:
  0.0 103.3 jit_solution(16969161462528607178)
XLA Ops:
  7.2 0.0 copy-start
  7.2 0.0 copy-start.2
  7.2 0.0 copy-start.3
  7.2 0.0 all-gather.4.cloned.1.call-start
  7.2 0.7 all-gather.4.cloned.1.call-update
  7.9 0.0 all-gather.6.cloned.1.call-start
  8.0 14.9 %all-gather.4.cloned.1.call-done = f32[64,8192]{1,0:T(8,128)} async-done(((f32[64,4096]{1,0:T(8,128)}), f32[64,8192]{1,0:T(8,128)}) %all-gather.4.cloned.1.call-update) | async-done | bytes 2097168 | tf_op jit(solution)/shard_map/all_gather | solution.py:23
  22.9 12.4 %fusion.4 = f32[64,256]{1,0:T(8,128)} fusion(f32[64,8192]{1,0:T(8,128)} %all-gather.4.cloned.1.call-done, f32[256,8192]{1,0:T(8,128)} %param.5), kind=kOutput, calls=%fused_computation.9 | convolution fusion | flops 1610612736 | bytes 10551296 | tf_op jit(solution)/shard_map/dot_general | solution.py:22
  35.3 0.0 all-gather.6.cloned.1.call-update
  35.3 56.4 %all-gather.6.cloned.1.call-done = f32[1024,256]{1,0:T(8,128)} async-done(((f32[64,256]{1,0:T(8,128)}), f32[1024,256]{1,0:T(8,128)}) %all-gather.6.cloned.1.call-update) | async-done | bytes 1048592 | tf_op jit(solution)/shard_map/all_gather | solution.py:8
  91.7 1.3 %reduce_sum.9 = f32[64,256]{1,0:T(8,128)S(1)} reduce(f32[16,64,256]{2,1,0:T(8,128)} %bitcast.3, f32[]{:T(128)} %constant.0.clone.1), dimensions={0}, to_apply=%region_0.0 | reduce | flops 245760 | bytes 1114116 | tf_op jit(solution)/shard_map/reduce_sum | solution.py:8
  93.0 0.0 copy-done
  93.0 0.0 copy-done.2
  93.0 0.0 copy-done.3
  93.0 0.2 abs_reduce_fusion
  93.2 0.0 copy-start.1
  93.2 2.5 %pmax.7 = f32[64]{0:T(128)S(1)} all-reduce(f32[64]{0:T(128)S(1)} %get-tuple-element.2), channel_id=1, replica_groups=mesh['col'=16,'row'=2] {'row'}, use_global_device_ids=true, to_apply=%region_2.0 | all-reduce | flops 64 | bytes 512 | tf_op jit(solution)/shard_map/pmax | solution.py:31
  95.7 0.7 multiply_add_fusion
  96.4 0.0 copy-done.1
  (1 shorter events, 0.0 us)
Async XLA Ops:
  7.2 85.9 %copy-start = (f32[64,256]{1,0:T(8,128)S(1)}, f32[64,256]{1,0:T(8,128)}, u32[]{:S(2)}) copy-start(f32[64,256]{1,0:T(8,128)} %param.9) | copy-start | bytes 196612
  7.2 85.9 %copy-start.2 = (f32[256]{0:T(256)S(1)}, f32[256]{0:T(256)}, u32[]{:S(2)}) copy-start(f32[256]{0:T(256)} %param.8) | copy-start | bytes 3076
  7.2 85.9 %copy-start.3 = (f32[256]{0:T(256)S(1)}, f32[256]{0:T(256)}, u32[]{:S(2)}) copy-start(f32[256]{0:T(256)} %param.7) | copy-start | bytes 3076
  7.2 15.7 %all-gather.4.cloned.1.call-start = ((), (), s32[]{:S(2)}) async-start(), calls=%async_computation | async-start | bytes 3145728 | tf_op jit(solution)/shard_map/all_gather | solution.py:23
  7.9 83.8 %all-gather.6.cloned.1.call-start = ((), (), s32[]{:S(2)}) async-start(), calls=%async_computation.1 | async-start | bytes 1114112 | tf_op jit(solution)/shard_map/all_gather | solution.py:8
  93.2 3.2 %copy-start.1 = (f32[64,256]{1,0:T(8,128)}, f32[64,256]{1,0:T(8,128)S(1)}, u32[]{:S(2)}) copy-start(f32[64,256]{1,0:T(8,128)S(1)} %get-tuple-element.3) | copy-start | bytes 196612
Sparse Core Ops, SparseCore 0:
  9.5 13.2 all-gather.3
  35.4 56.2 all-gather.5
